TPU v7x, 32 devices: a whole 2x2x4 slice. The times are simulated.
32 devices in a mesh: section: 4 (over x, core), fsdp: 8 (over z, y).
Axes of the slice: x: 2, y: 2, z: 4, core: 2. Of those that a mesh axis runs over, the one named last changes fastest.
Arguments:
- tokens: bfloat16 [4, 2, 1024, 8192], P('section', None, 'fsdp'), may hold values from -6 to 6
- queries: bfloat16 [4, 2, 1024, 4096], P('section', None, 'fsdp'), may hold values from -200 to 200
- gains: bfloat16 [4, 8192], P('section'), may hold values from 0.5 to 1.5
- key_weight: bfloat16 [4, 8192, 512], P('section', 'fsdp'), may hold values from -0.0625 to 0.0625
- value_weight: bfloat16 [4, 8192, 512], P('section', 'fsdp'), may hold values from -0.0625 to 0.0625
- lengths: int32 [2, 16], replicated, may hold values from 1 to 128, 1024 in all within a row
Outputs:
- attended: bfloat16 [4, 2, 1024, 4096], P('section', None, 'fsdp')
Inputs may be any that keep to these rules, and one draw needn't show every extreme that they name: `lengths`: each row sums to 1024; some document has exactly 128 tokens.
All inputs are finite; a program needn't handle non-finite values.
Results may differ from a plain program's by a relative error of at most 0.012.
The roundings to bfloat16 on the way count: a program that leaves them out, or rounds other values in their place, can miss the bound.
Values may be sent and summed in bfloat16 or wider, within the bound.
A program may use at most 128 MiB of HBM per device.

v0:
```python
import functools

import jax
import jax.numpy as jnp
from jax import lax
from jax.experimental import pallas as pl
from jax.experimental.pallas import tpu as pltpu
from jax.sharding import PartitionSpec as P

HEAD = 128
AXIS = "fsdp"


def kernel(
    n,
    x_hbm, q_hbm, gain_ref, kw_hbm, vw_hbm, len_ref, o_hbm,
    x_v, q_v, o_v, wbuf, xs, sx, pk_s, pk_r, pv_s, pv_r, own_acc, kv, prior, start_s,
    lw_sem, lx_sem, lq_sem, lo_sem,
    ws_sem, wr_sem, ys_sem, yr_sem, xs_sem, xr_sem, ps_sem, pr_sem, ks_sem, kr_sem,
):
    slots, tok, depth = x_v.shape
    chunks, groups, _, rows, _ = wbuf.shape
    wide = 2 * rows
    total = slots * tok
    q_per_kv = q_v.shape[2] // (chunks * HEAD)
    me = lax.axis_index(AXIS)
    bit = me % 2
    cls = (me // 2) % 2
    grp = me // 4
    y_peer = me + 1 - 2 * bit
    z_peer = me + 2 - 4 * cls
    right = lax.rem(me + 1, n)
    left = lax.rem(me + n - 1, n)
    others = [lax.rem(grp + d, groups) for d in range(1, groups)]

    def dev(g):
        return g * 4 + cls * 2 + bit

    def load_w(c):
        cols = pl.ds(c * HEAD, HEAD)
        return [
            pltpu.make_async_copy(
                w.at[0, :, cols], wbuf.at[c, grp, bit, :, pl.ds(i * HEAD, HEAD)], lw_sem.at[c, i]
            )
            for i, w in enumerate((kw_hbm, vw_hbm))
        ]

    x_loads = [pltpu.make_async_copy(x_hbm.at[0, s], x_v.at[s], lx_sem.at[s]) for s in range(slots)]
    q_load = pltpu.make_async_copy(q_hbm.at[0], q_v, lq_sem)
    w_loads = [load_w(c) for c in range(chunks)]
    for copy in w_loads[0] + x_loads:
        copy.start()
    for c in range(1, chunks):
        for copy in w_loads[c]:
            copy.start()
    q_load.start()

    prior[...] = jnp.zeros_like(prior)

    barrier = pltpu.get_barrier_semaphore()
    peers = [y_peer, z_peer, right, left] + [dev(g) for g in others]
    for peer in peers:
        pl.semaphore_signal(barrier, inc=1, device_id={AXIS: peer}, device_id_type=pl.DeviceIdType.MESH)
    pl.semaphore_wait(barrier, len(peers))

    def remote(src, dst, send, recv, peer):
        return pltpu.make_async_remote_copy(
            src_ref=src, dst_ref=dst, send_sem=send, recv_sem=recv,
            device_id={AXIS: peer}, device_id_type=pl.DeviceIdType.MESH,
        )

    def w_copy(c, source_grp, index_grp, peer):
        block = wbuf.at[c, source_grp, bit]
        return remote(block, block, ws_sem.at[c, index_grp], wr_sem.at[c, source_grp], peer)

    def y_copy(c, g, side):
        block = wbuf.at[c, g, side]
        return remote(block, block, ys_sem.at[c, g], yr_sem.at[c, g], y_peer)

    outer = cls == grp % 2

    def send_w(c):
        for copy in w_loads[c]:
            copy.wait()
        for g in others:
            w_copy(c, grp, g, dev(g)).start()
        y_copy(c, grp, bit).start()

    def x_copy(s, g):
        return remote(
            sx.at[g, pl.ds(s * tok, tok)], xs.at[g, pl.ds(total + s * tok, tok)],
            xs_sem.at[s, g], xr_sem.at[s, g], z_peer,
        )

    def p_copies(c):
        return [
            remote(src.at[c], dst.at[c], ps_sem.at[c, i], pr_sem.at[c, i], z_peer)
            for i, (src, dst) in enumerate(((pk_s, pk_r), (pv_s, pv_r)))
        ]

    def k_copy(c):
        return remote(kv.at[c], prior.at[c], ks_sem.at[c], kr_sem.at[c], right)

    @pl.when(jnp.logical_not(outer))
    def _():
        send_w(0)

    block_rows = 16

    def norm_block(s, r):
        here = pl.ds(pl.multiple_of(r * block_rows, block_rows), block_rows)
        there = pl.ds(pl.multiple_of(s * tok + r * block_rows, block_rows), block_rows)
        squares = jnp.zeros((block_rows, 1), jnp.float32)
        step = 2 * wide
        for i in range(depth // step):
            piece = x_v[s, here, i * step:(i + 1) * step].astype(jnp.float32)
            squares = squares + jnp.sum(piece * piece, axis=-1, keepdims=True)
        inverse = lax.rsqrt(squares / depth + 1e-05)
        for g in range(groups):
            for mine in (True, False):
                first = (4 * g + 2 * (cls if mine else 1 - cls)) * rows
                cols = pl.ds(pl.multiple_of(first, HEAD), wide)
                value = x_v[s, here, cols].astype(jnp.float32) * inverse
                value = (value * gain_ref[0:1, cols].astype(jnp.float32)).astype(jnp.bfloat16)
                if mine:
                    xs[g, there, :] = value
                else:
                    sx[g, there, :] = value

    for s in range(slots):
        x_loads[s].wait()

        def norm_step(r, carry, s=s):
            norm_block(s, r)
            return carry

        lax.fori_loop(0, tok // block_rows, norm_step, 0)
        @pl.when(outer)
        def _(s=s):
            for g in range(groups):
                x_copy(s, g).start()

    @pl.when(outer)
    def _():
        send_w(0)

    for c in range(1, chunks):
        send_w(c)

    docs = len_ref.shape[1]
    rowi = lax.broadcasted_iota(jnp.int32, (docs, docs), 0)
    coli = lax.broadcasted_iota(jnp.int32, (docs, docs), 1)
    pos = lax.broadcasted_iota(jnp.int32, (tok, 1), 0) + me * tok
    for s in range(slots):
        lens = jnp.broadcast_to(len_ref[s:s + 1, :], (docs, docs))
        bounds = jnp.sum(jnp.where(coli <= rowi, lens, 0), axis=1, keepdims=True)
        bound_row = jnp.sum(jnp.where(coli == rowi, bounds, 0), axis=0, keepdims=True)
        start = jnp.max(jnp.where(bound_row <= pos, bound_row, 0), axis=1, keepdims=True)
        start_s[s] = jnp.broadcast_to(start, (tok, HEAD))
    q_load.wait()

    @pl.when(jnp.logical_not(outer))
    def _():
        for c in range(chunks):
            for g in others:
                w_copy(c, grp, g, dev(g)).wait_send()
        for s in range(slots):
            for g in range(groups):
                x_copy(s, g).start()

    def forward(c):
        for g in others:
            w_copy(c, g, g, dev(g)).wait_recv()
            y_copy(c, g, bit).start()

    def project(c, lo):
        acc = jnp.zeros((total, 2 * HEAD), jnp.float32)
        for g in range(groups):
            acc = acc + jnp.dot(
                xs[g, lo:lo + total, :], wbuf[c, g].reshape(wide, 2 * HEAD),
                preferred_element_type=jnp.float32,
            )
        return acc

    def own_rows(c):
        own_acc[c] = project(c, 0)

    def y_wait(c):
        for g in range(groups):
            y_copy(c, g, 1 - bit).wait_recv()

    @pl.when(outer)
    def _():
        for c in range(chunks):
            forward(c)
        for c in range(chunks):
            y_wait(c)
            own_rows(c)

    def stage_a(c):
        @pl.when(jnp.logical_not(outer))
        def _():
            if c == 0:
                forward(0)
            if c + 1 < chunks:
                forward(c + 1)
            y_wait(c)

        if c == 0:
            for s in range(slots):
                for g in range(groups):
                    x_copy(s, g).wait_recv()
        partial = project(c, total)
        pk_s[c] = partial[:, :HEAD]
        pv_s[c] = partial[:, HEAD:].astype(jnp.bfloat16)
        for copy in p_copies(c):
            copy.start()

        @pl.when(jnp.logical_not(outer))
        def _():
            own_rows(c)

    def stage_b(c):
        for copy in p_copies(c):
            copy.wait_recv()
        kv[c, :, 0:HEAD] = (own_acc[c, :, 0:HEAD] + pk_r[c]).astype(jnp.bfloat16)
        kv[c, :, HEAD:] = (own_acc[c, :, HEAD:] + pv_r[c].astype(jnp.float32)).astype(jnp.bfloat16)

        @pl.when(me < n - 1)
        def _():
            k_copy(c).start()

    key_pos = lax.broadcasted_iota(jnp.int32, (tok, 2 * tok), 1) + (me - 1) * tok
    query_pos = lax.broadcasted_iota(jnp.int32, (tok, 2 * tok), 0) + me * tok

    def out_copy(c):
        cols = pl.ds(c * q_per_kv * HEAD, q_per_kv * HEAD)
        return pltpu.make_async_copy(o_v.at[:, :, cols], o_hbm.at[0, :, :, cols], lo_sem.at[c])

    def stage_c(c):
        @pl.when(me > 0)
        def _():
            k_copy(c).wait_recv()

        for s in range(slots):
            here = slice(s * tok, (s + 1) * tok)
            keys = jnp.concatenate([prior[c, here, 0:HEAD], kv[c, here, 0:HEAD]], axis=0)
            values = jnp.concatenate([prior[c, here, HEAD:], kv[c, here, HEAD:]], axis=0)
            allowed = (key_pos >= start_s[s][:, 0:1]) & (key_pos <= query_pos)

            def head_step(h, carry, s=s, keys=keys, values=values, allowed=allowed):
                cols = pl.ds(pl.multiple_of((c * q_per_kv + h) * HEAD, HEAD), HEAD)
                scores = lax.dot_general(
                    q_v[s, :, cols], keys, (((1,), (1,)), ((), ())),
                    preferred_element_type=jnp.float32,
                ) * HEAD ** (-0.5)
                scores = jnp.where(allowed, scores, -1e30)
                maxima = jnp.max(scores, axis=-1, keepdims=True)
                exponent = jnp.where(allowed, jnp.exp(scores - maxima), 0.0)
                sums = jnp.sum(exponent, axis=-1, keepdims=True)
                soft = (exponent / sums).astype(jnp.bfloat16)
                mixed = jnp.dot(soft, values, preferred_element_type=jnp.float32)
                o_v[s, :, cols] = mixed.astype(jnp.bfloat16)
                return carry

            lax.fori_loop(0, q_per_kv, head_step, 0, unroll=True)
        out_copy(c).start()

    for c in range(chunks - 1):
        stage_a(c)
    stage_b(0)
    stage_b(1)
    stage_a(chunks - 1)
    for c in range(2, chunks):
        stage_c(c - 2)
        stage_b(c)
    stage_c(chunks - 2)
    stage_c(chunks - 1)

    for c in range(chunks):
        out_copy(c).wait()
        @pl.when(outer)
        def _(c=c):
            for g in others:
                w_copy(c, grp, g, dev(g)).wait_send()

        for g in range(groups):
            y_copy(c, g, bit).wait_send()
        for copy in p_copies(c):
            copy.wait_send()

        @pl.when(me < n - 1)
        def _(c=c):
            k_copy(c).wait_send()

    for s in range(slots):
        for g in range(groups):
            x_copy(s, g).wait_send()


def body(tokens, queries, gains, key_weight, value_weight, lengths):
    n = lax.axis_size(AXIS)
    _, slots, tok, depth = tokens.shape
    _, rows, key_width = key_weight.shape
    chunks = key_width // HEAD
    groups = n // 4
    total = slots * tok
    bf, f32 = jnp.bfloat16, jnp.float32
    any_spec = pl.BlockSpec(memory_space=pl.ANY)
    vmem_spec = pl.BlockSpec(memory_space=pltpu.VMEM)
    dma = pltpu.SemaphoreType.DMA
    return pl.pallas_call(
        functools.partial(kernel, n),
        out_shape=jax.ShapeDtypeStruct(queries.shape, bf),
        in_specs=[any_spec, any_spec, vmem_spec, any_spec, any_spec, vmem_spec],
        out_specs=any_spec,
        scratch_shapes=[
            pltpu.VMEM((slots, tok, depth), bf),
            pltpu.VMEM(queries.shape[1:], bf),
            pltpu.VMEM(queries.shape[1:], bf),
            pltpu.VMEM((chunks, groups, 2, rows, 2 * HEAD), bf),
            pltpu.VMEM((groups, 2 * total, 2 * rows), bf),
            pltpu.VMEM((groups, total, 2 * rows), bf),
            pltpu.VMEM((chunks, total, HEAD), f32),
            pltpu.VMEM((chunks, total, HEAD), f32),
            pltpu.VMEM((chunks, total, HEAD), bf),
            pltpu.VMEM((chunks, total, HEAD), bf),
            pltpu.VMEM((chunks, total, 2 * HEAD), f32),
            pltpu.VMEM((chunks, total, 2 * HEAD), bf),
            pltpu.VMEM((chunks, total, 2 * HEAD), bf),
            pltpu.VMEM((slots, tok, HEAD), jnp.int32),
            dma((chunks, 2)), dma((slots,)), dma, dma((chunks,)),
            dma((chunks, groups)), dma((chunks, groups)),
            dma((chunks, groups)), dma((chunks, groups)),
            dma((slots, groups)), dma((slots, groups)),
            dma((chunks, 2)), dma((chunks, 2)), dma((chunks,)), dma((chunks,)),
        ],
        compiler_params=pltpu.CompilerParams(
            collective_id=0, has_side_effects=True, vmem_limit_bytes=60 * 1024 * 1024
        ),
    )(tokens, queries, gains, key_weight, value_weight, lengths)


def solution(mesh):
    return jax.shard_map(
        body,
        mesh=mesh,
        in_specs=(
            P("section", None, "fsdp", None),
            P("section", None, "fsdp", None),
            P("section", None),
            P("section", "fsdp", None),
            P("section", "fsdp", None),
            P(),
        ),
        out_specs=P("section", None, "fsdp", None),
        check_vma=False,
    )
```

profile of v0, /device:TPU:8, one launch (start us, length us, event | category | flops | bytes accessed | tf_op | source)
XLA Modules:
  0.0 136.3 jit_solution(15436604346113700235)
XLA Ops:
  0.0 133.2 %shard_map.64 = bf16[1,2,128,4096]{3,2,1,0:T(8,128)(2,1)} custom-call(bf16[1,2,128,8192]{3,2,1,0:T(8,128)(2,1)} %x_hbm.1, bf16[1,2,128,4096]{3,2,1,0:T(8,128)(2,1)} %q_hbm.1, bf16[1,8192]{1,0:T(2,128)(2,1)} %gain_ref.1, bf16[1,1024,512]{2,1,0:T(8,128)(2,1)} %kw_hbm.1, bf16[1,1024,512]{2,1,0:T(8,128)(2,1)} %vw_hbm.1, s32[2,16]{1,0:T(2,128)} %len_ref.1), custom_call_target="tpu_custom_call" | custom-call | tf_op jit(solution)/shard_map/pallas_call | solution.py:312
  133.2 3.1 %copy.8 = bf16[1,2,128,4096]{3,2,1,0:T(8,128)(2,1)} copy(bf16[1,2,128,4096]{3,2,1,0:T(8,128)(2,1)} %shard_map.64) | data formatting | bytes 4194304
where the time goes:
time: 137 us; the launch traced here: 136 us
  Pallas kernels  133 us (97%)
  local copies, waits for them, and re-layouts  3.13 us (2%)
    pallas_call x1, Pallas kernels, body(): pl.pallas_call(functools.partial(kernel, n), out_shape=jax.ShapeDtypeStru...  133 us
    unnamed x1, local copies, waits for them, and re-layouts  3.13 us

commit v1 on v0

v1 whole, which is shorter than its diff:
```python
import functools

import jax
import jax.numpy as jnp
from jax import lax
from jax.experimental import pallas as pl
from jax.experimental.pallas import tpu as pltpu
from jax.sharding import PartitionSpec as P

HEAD = 128
AXIS = "fsdp"
LEAD = 2


def kernel(
    n, keep,
    x_hbm, q_hbm, gain_ref, kw_hbm, vw_hbm, len_ref, o_hbm,
    x_v, q_v, o_v, wbuf, xs, sx, lx, acc, zs, zr, ys, yr, kv, prior, start_s,
    lw_sem, lx_sem, lq_sem, lo_sem,
    wz_s, wz_r, wh_s, wh_r, wk_s, wk_r, xy_s, xy_r, xz_s, xz_r,
    z_s, z_r, y_s, y_r, p_s, p_r,
):
    slots, tok, depth = x_v.shape
    pieces, groups, _, rows, _ = wbuf.shape
    heads = pieces // 2
    total = slots * tok
    q_per_kv = q_v.shape[2] // (heads * HEAD)
    me = lax.axis_index(AXIS)
    bit = me % 2
    cls = (me // 2) % 2
    grp = me // 4
    leaf = cls == grp % 2
    hub = jnp.logical_not(leaf)
    kind = jnp.where(leaf, 1, 0)
    y_peer = me + 1 - 2 * bit
    z_peer = me + 2 - 4 * cls
    right = lax.rem(me + 1, n)
    left = lax.rem(me + n - 1, n)
    others = [lax.rem(grp + d, groups) for d in range(1, groups)]
    span = range(len(others))

    def hub_of(g):
        return 4 * g + 2 * (1 - g % 2) + bit

    def load_w(j):
        w = vw_hbm if j % 2 else kw_hbm
        cols = pl.ds((j // 2) * HEAD, HEAD)
        return pltpu.make_async_copy(w.at[0, :, cols], wbuf.at[j, grp, kind], lw_sem.at[j])

    x_loads = [pltpu.make_async_copy(x_hbm.at[0, s], x_v.at[s], lx_sem.at[s]) for s in range(slots)]
    q_load = pltpu.make_async_copy(q_hbm.at[0], q_v, lq_sem)
    w_loads = [load_w(j) for j in range(pieces)]
    for copy in w_loads[:2] + x_loads[:1] + w_loads[2:] + x_loads[1:] + [q_load]:
        copy.start()

    barrier = pltpu.get_barrier_semaphore()

    def greet(peer):
        pl.semaphore_signal(barrier, inc=1, device_id={AXIS: peer}, device_id_type=pl.DeviceIdType.MESH)

    greet(y_peer)
    greet(z_peer)

    @pl.when(hub)
    def _():
        for g in others:
            greet(hub_of(g))

    @pl.when(me < n - 1)
    def _():
        greet(right)

    @pl.when(me > 0)
    def _():
        greet(left)

    prior[...] = jnp.zeros_like(prior)
    pl.semaphore_wait(
        barrier,
        2 + jnp.where(hub, len(others), 0) + jnp.where(me < n - 1, 1, 0) + jnp.where(me > 0, 1, 0),
    )

    def remote(src, dst, send, recv, peer):
        return pltpu.make_async_remote_copy(
            src_ref=src, dst_ref=dst, send_sem=send, recv_sem=recv,
            device_id={AXIS: peer}, device_id_type=pl.DeviceIdType.MESH,
        )

    def w_pair(j, k):
        block = wbuf.at[j, grp, k]
        return remote(block, block, wz_s.at[j], wz_r.at[j], z_peer)

    def w_hub(j, k, d, g):
        block = wbuf.at[j, g, k]
        return remote(block, block, wh_s.at[j, k, d], wh_r.at[j, k, g], hub_of(others[d]))

    def w_keep(j, d):
        block = wbuf.at[j, others[d], 0, pl.ds(0, keep)]
        return remote(block, block, wk_s.at[j, d], wk_r.at[j, d], z_peer)

    def x_y(s, g, k):
        return remote(
            sx.at[g, k, pl.ds(s * tok, tok)], xs.at[g, k, pl.ds(total + s * tok, tok)],
            xy_s.at[s, g, k], xy_r.at[s, g, k], y_peer,
        )

    def x_z(p, d, k):
        skip = 0 if k else keep
        here = (others[d], k, pl.ds(p * tok, tok), pl.ds(skip, rows - skip))
        return remote(xs.at[here], lx.at[here], xz_s.at[p, d, k], xz_r.at[p, d, k], z_peer)

    def z_copy(j):
        return remote(zs.at[j], zr.at[j], z_s.at[j], z_r.at[j], z_peer)

    def y_copy(j):
        return remote(ys.at[j], yr.at[j], y_s.at[j], y_r.at[j], y_peer)

    def p_copy(j):
        return remote(kv.at[j], prior.at[j], p_s.at[j], p_r.at[j], right)

    for j in range(pieces):
        w_loads[j].wait()

        @pl.when(hub)
        def _(j=j):
            w_pair(j, 0).start()
            for d in span:
                w_hub(j, 0, d, grp).start()

        if j < LEAD:
            @pl.when(leaf)
            def _(j=j):
                w_pair(j, 1).start()

    block_rows = 16

    def norm_block(s, r):
        here = pl.ds(pl.multiple_of(r * block_rows, block_rows), block_rows)
        there = pl.ds(pl.multiple_of(s * tok + r * block_rows, block_rows), block_rows)
        squares = jnp.zeros((block_rows, 1), jnp.float32)
        step = 4 * HEAD
        for i in range(depth // step):
            piece = x_v[s, here, i * step:(i + 1) * step].astype(jnp.float32)
            squares = squares + jnp.sum(piece * piece, axis=-1, keepdims=True)
        inverse = lax.rsqrt(squares / depth + 1e-05)
        for g in range(groups):
            for k in range(2):
                line = g % 2 if k else 1 - g % 2
                for mine in (False, True):
                    first = (4 * g + 2 * line + (bit if mine else 1 - bit)) * rows
                    cols = pl.ds(pl.multiple_of(first, HEAD), rows)
                    value = x_v[s, here, cols].astype(jnp.float32) * inverse
                    value = (value * gain_ref[0:1, cols].astype(jnp.float32)).astype(jnp.bfloat16)
                    if mine:
                        xs[g, k, there, :] = value
                    else:
                        sx[g, k, there, :] = value

    for s in range(slots):
        x_loads[s].wait()

        def norm_step(r, carry, s=s):
            norm_block(s, r)
            return carry

        lax.fori_loop(0, tok // block_rows, norm_step, 0)
        for g in others + [grp]:
            for k in range(2):
                x_y(s, g, k).start()

        @pl.when(leaf)
        def _(s=s):
            for d in span:
                for k in range(2):
                    x_z(s, d, k).start()

    docs = len_ref.shape[1]
    rowi = lax.broadcasted_iota(jnp.int32, (docs, docs), 0)
    coli = lax.broadcasted_iota(jnp.int32, (docs, docs), 1)
    pos = lax.broadcasted_iota(jnp.int32, (tok, 1), 0) + me * tok
    for s in range(slots):
        lens = jnp.broadcast_to(len_ref[s:s + 1, :], (docs, docs))
        bounds = jnp.sum(jnp.where(coli <= rowi, lens, 0), axis=1, keepdims=True)
        bound_row = jnp.sum(jnp.where(coli == rowi, bounds, 0), axis=0, keepdims=True)
        start = jnp.max(jnp.where(bound_row <= pos, bound_row, 0), axis=1, keepdims=True)
        start_s[s] = jnp.broadcast_to(start, (tok, HEAD))
    q_load.wait()

    def dot(a, b):
        return jnp.dot(a, b, preferred_element_type=jnp.float32)

    def loop(lo, hi, step):
        def run(j, carry):
            step(j)
            return carry

        lax.fori_loop(lo, hi, run, 0)

    def take_hub(j):
        for d in span:
            w_hub(j, 0, d, others[d]).wait_recv()
            if keep:
                w_keep(j, d).start()

    def pass_leaf(j):
        w_pair(j, 1).wait_recv()
        for d in span:
            w_hub(j, 1, d, grp).start()

    @pl.when(hub)
    def _():
        loop(0, pieces // 2, take_hub)
        loop(0, LEAD, pass_leaf)
        loop(pieces // 2, pieces, take_hub)
        pass_leaf(LEAD)
        for s in range(slots):
            for g in others + [grp]:
                for k in range(2):
                    x_y(s, g, k).wait_recv()

        def first(j):
            value = dot(xs[grp, 0], wbuf[j, grp, 0])
            for g in others:
                value = value + dot(xs[g, 0], wbuf[j, g, 0])
            acc[j] = value

        loop(0, pieces, first)
        for p in range(2 * slots):
            for d in span:
                for k in range(2):
                    x_z(p, d, k).wait_recv()

    @pl.when(leaf)
    def _():
        for s in range(slots):
            for d in span:
                for k in range(2):
                    x_y(s, others[d], k).wait_recv()
                    x_z(slots + s, d, k).start()

        def send_w(j):
            w_pair(j, 1).start()

        loop(LEAD, pieces, send_w)
        for s in range(slots):
            for k in range(2):
                x_y(s, grp, k).wait_recv()

        def first(j):
            w_pair(j, 0).wait_recv()
            acc[j] = dot(xs[grp, 0], wbuf[j, grp, 0]) + dot(xs[grp, 1], wbuf[j, grp, 1])

        loop(0, pieces, first)
        if keep:
            def second(j):
                value = acc[j]
                for d in span:
                    w_keep(j, d).wait_recv()
                    value = value + dot(
                        xs[others[d], 0, :, 0:keep], wbuf[j, others[d], 0, 0:keep]
                    )
                acc[j] = value

            loop(0, pieces, second)

    def meet(j):
        @pl.when(hub)
        def _():
            for d in span:
                w_hub(j, 1, d, others[d]).wait_recv()
            value = jnp.zeros((2 * total, HEAD), jnp.float32)
            for g in others:
                value = value + dot(lx[g, 0, :, keep:], wbuf[j, g, 0, keep:])
                value = value + dot(lx[g, 1], wbuf[j, g, 1])
            zs[j] = value.astype(jnp.bfloat16)
            z_copy(j).start()
            value = acc[j] + dot(xs[grp, 1], wbuf[j, grp, 1])
            for g in others:
                value = value + dot(xs[g, 1], wbuf[j, g, 1])
            acc[j] = value
            ys[j] = value[total:].astype(jnp.bfloat16)
            y_copy(j).start()

            @pl.when(j + LEAD + 1 < pieces)
            def _():
                pass_leaf(j + LEAD + 1)

        @pl.when(leaf)
        def _():
            z_copy(j).wait_recv()
            value = acc[j] + zr[j].astype(jnp.float32)
            acc[j] = value
            ys[j] = value[total:].astype(jnp.bfloat16)
            y_copy(j).start()

    def finish(j):
        y_copy(j).wait_recv()
        kv[j] = (acc[j, 0:total] + yr[j].astype(jnp.float32)).astype(jnp.bfloat16)

        @pl.when(me < n - 1)
        def _():
            p_copy(j).start()

    key_pos = lax.broadcasted_iota(jnp.int32, (tok, 2 * tok), 1) + (me - 1) * tok
    query_pos = lax.broadcasted_iota(jnp.int32, (tok, 2 * tok), 0) + me * tok
    wide = q_per_kv * HEAD

    def out_copy(h):
        cols = pl.ds(pl.multiple_of(h * wide, HEAD), wide)
        return pltpu.make_async_copy(o_v.at[:, :, cols], o_hbm.at[0, :, :, cols], lo_sem.at[h])

    def attend(h):
        @pl.when(me > 0)
        def _():
            p_copy(2 * h).wait_recv()
            p_copy(2 * h + 1).wait_recv()

        for s in range(slots):
            here = slice(s * tok, (s + 1) * tok)
            keys = jnp.concatenate([prior[2 * h, here], kv[2 * h, here]], axis=0)
            values = jnp.concatenate([prior[2 * h + 1, here], kv[2 * h + 1, here]], axis=0)
            allowed = (key_pos >= start_s[s][:, 0:1]) & (key_pos <= query_pos)
            for q in range(q_per_kv):
                cols = pl.ds(pl.multiple_of((h * q_per_kv + q) * HEAD, HEAD), HEAD)
                scores = lax.dot_general(
                    q_v[s, :, cols], keys, (((1,), (1,)), ((), ())),
                    preferred_element_type=jnp.float32,
                ) * HEAD ** (-0.5)
                scores = jnp.where(allowed, scores, -1e30)
                maxima = jnp.max(scores, axis=-1, keepdims=True)
                exponent = jnp.where(allowed, jnp.exp(scores - maxima), 0.0)
                sums = jnp.sum(exponent, axis=-1, keepdims=True)
                soft = (exponent / sums).astype(jnp.bfloat16)
                o_v[s, :, cols] = dot(soft, values).astype(jnp.bfloat16)
        out_copy(h).start()

    def round_of(h):
        meet(2 * h)
        finish(2 * h)
        meet(2 * h + 1)

        @pl.when(h > 0)
        def _():
            attend(h - 1)

        finish(2 * h + 1)

    loop(0, heads, round_of)
    attend(heads - 1)

    def drain(j):
        y_copy(j).wait_send()

        @pl.when(me < n - 1)
        def _():
            p_copy(j).wait_send()

        @pl.when(hub)
        def _():
            w_pair(j, 0).wait_send()
            z_copy(j).wait_send()
            for d in span:
                w_hub(j, 0, d, grp).wait_send()
                w_hub(j, 1, d, grp).wait_send()
                if keep:
                    w_keep(j, d).wait_send()

        @pl.when(leaf)
        def _():
            w_pair(j, 1).wait_send()

    loop(0, pieces, drain)
    for s in range(slots):
        for g in range(groups):
            for k in range(2):
                x_y(s, g, k).wait_send()

    @pl.when(leaf)
    def _():
        for p in range(2 * slots):
            for d in span:
                for k in range(2):
                    x_z(p, d, k).wait_send()

    for h in range(heads):
        out_copy(h).wait()


def body(tokens, queries, gains, key_weight, value_weight, lengths):
    n = lax.axis_size(AXIS)
    _, slots, tok, depth = tokens.shape
    _, rows, key_width = key_weight.shape
    heads = key_width // HEAD
    pieces = 2 * heads
    groups = n // 4
    total = slots * tok
    keep = rows // 2 // HEAD * HEAD
    bf, f32 = jnp.bfloat16, jnp.float32
    any_spec = pl.BlockSpec(memory_space=pl.ANY)
    vmem_spec = pl.BlockSpec(memory_space=pltpu.VMEM)
    dma = pltpu.SemaphoreType.DMA
    fan = groups - 1
    return pl.pallas_call(
        functools.partial(kernel, n, keep),
        out_shape=jax.ShapeDtypeStruct(queries.shape, bf),
        in_specs=[any_spec, any_spec, vmem_spec, any_spec, any_spec, vmem_spec],
        out_specs=any_spec,
        scratch_shapes=[
            pltpu.VMEM((slots, tok, depth), bf),
            pltpu.VMEM(queries.shape[1:], bf),
            pltpu.VMEM(queries.shape[1:], bf),
            pltpu.VMEM((pieces, groups, 2, rows, HEAD), bf),
            pltpu.VMEM((groups, 2, 2 * total, rows), bf),
            pltpu.VMEM((groups, 2, total, rows), bf),
            pltpu.VMEM((groups, 2, 2 * total, rows), bf),
            pltpu.VMEM((pieces, 2 * total, HEAD), f32),
            pltpu.VMEM((pieces, 2 * total, HEAD), bf),
            pltpu.VMEM((pieces, 2 * total, HEAD), bf),
            pltpu.VMEM((pieces, total, HEAD), bf),
            pltpu.VMEM((pieces, total, HEAD), bf),
            pltpu.VMEM((pieces, total, HEAD), bf),
            pltpu.VMEM((pieces, total, HEAD), bf),
            pltpu.VMEM((slots, tok, HEAD), jnp.int32),
            dma((pieces,)), dma((slots,)), dma, dma((heads,)),
            dma((pieces,)), dma((pieces,)),
            dma((pieces, 2, fan)), dma((pieces, 2, groups)),
            dma((pieces, fan)), dma((pieces, fan)),
            dma((slots, groups, 2)), dma((slots, groups, 2)),
            dma((2 * slots, fan, 2)), dma((2 * slots, fan, 2)),
            dma((pieces,)), dma((pieces,)),
            dma((pieces,)), dma((pieces,)),
            dma((pieces,)), dma((pieces,)),
        ],
        compiler_params=pltpu.CompilerParams(
            collective_id=0, has_side_effects=True, vmem_limit_bytes=60 * 1024 * 1024
        ),
    )(tokens, queries, gains, key_weight, value_weight, lengths)


def solution(mesh):
    return jax.shard_map(
        body,
        mesh=mesh,
        in_specs=(
            P("section", None, "fsdp", None),
            P("section", None, "fsdp", None),
            P("section", None),
            P("section", "fsdp", None),
            P("section", "fsdp", None),
            P(),
        ),
        out_specs=P("section", None, "fsdp", None),
        check_vma=False,
    )
```

time: 137 us -> 125 us (0.912)
  Pallas kernels: 133 us -> 120 us
    pallas_call x1, Pallas kernels: 133 us -> 120 us  [body(): pl.pallas_call(functools.partial(kernel, n, keep), out_shape=jax.ShapeDty...]
where the time goes in v1:
time: 125 us; the launch traced here: 123 us
  Pallas kernels  120 us (96%)
  local copies, waits for them, and re-layouts  3.13 us (3%)
    pallas_call x1, Pallas kernels, body(): pl.pallas_call(functools.partial(kernel, n, keep), out_shape=jax.ShapeDty...  120 us
    unnamed x1, local copies, waits for them, and re-layouts  3.13 us

profile of v1, /device:TPU:8, one launch (start us, length us, event | category | flops | bytes accessed | tf_op | source)
XLA Modules:
  0.0 123.2 jit_solution(2783828435589791283)
XLA Ops:
  0.0 120.1 %shard_map.64 = bf16[1,2,128,4096]{3,2,1,0:T(8,128)(2,1)} custom-call(bf16[1,2,128,8192]{3,2,1,0:T(8,128)(2,1)} %x_hbm.1, bf16[1,2,128,4096]{3,2,1,0:T(8,128)(2,1)} %q_hbm.1, bf16[1,8192]{1,0:T(2,128)(2,1)} %gain_ref.1, bf16[1,1024,512]{2,1,0:T(8,128)(2,1)} %kw_hbm.1, bf16[1,1024,512]{2,1,0:T(8,128)(2,1)} %vw_hbm.1, s32[2,16]{1,0:T(2,128)} %len_ref.1), custom_call_target="tpu_custom_call" | custom-call | tf_op jit(solution)/shard_map/pallas_call | solution.py:403
  120.1 3.1 %copy.8 = bf16[1,2,128,4096]{3,2,1,0:T(8,128)(2,1)} copy(bf16[1,2,128,4096]{3,2,1,0:T(8,128)(2,1)} %shard_map.64) | data formatting | bytes 4194304

commit v2 on v1

--- a/solution.py
+++ b/solution.py
@@ -10,15 +10,17 @@
 HEAD = 128
 AXIS = "fsdp"
 LEAD = 2
+LAG = 2
+EARLY = 2
 
 
 def kernel(
     n, keep,
     x_hbm, q_hbm, gain_ref, kw_hbm, vw_hbm, len_ref, o_hbm,
-    x_v, q_v, o_v, wbuf, xs, sx, lx, acc, zs, zr, ys, yr, kv, prior, start_s,
+    x_v, q_v, o_v, wbuf, xs, sx, lx, acc, ls, lr, zs, zr, ys, yr, es, er, kv, kx, prior, side, weights, start_s,
     lw_sem, lx_sem, lq_sem, lo_sem,
     wz_s, wz_r, wh_s, wh_r, wk_s, wk_r, xy_s, xy_r, xz_s, xz_r,
-    z_s, z_r, y_s, y_r, p_s, p_r,
+    l_s, l_r, z_s, z_r, y_s, y_r, e_s, e_r, p_s, p_r, r_s,
 ):
     slots, tok, depth = x_v.shape
     pieces, groups, _, rows, _ = wbuf.shape
@@ -38,6 +40,9 @@
     left = lax.rem(me + n - 1, n)
     others = [lax.rem(grp + d, groups) for d in range(1, groups)]
     span = range(len(others))
+    cross = (me % 4 == 3) & (grp % 2 == 0) & (me < n - 1)
+    relay = (me % 4 == 2) & (grp % 2 == 0) & (me < n - 2)
+    far = (me % 4 == 0) & (grp % 2 == 1)
 
     def hub_of(g):
         return 4 * g + 2 * (1 - g % 2) + bit
@@ -70,6 +75,14 @@
     def _():
         greet(right)
 
+    @pl.when(relay)
+    def _():
+        greet(lax.rem(me + 2, n))
+
+    @pl.when(far)
+    def _():
+        greet(me - 2)
+
     @pl.when(me > 0)
     def _():
         greet(left)
@@ -77,7 +90,8 @@
     prior[...] = jnp.zeros_like(prior)
     pl.semaphore_wait(
         barrier,
-        2 + jnp.where(hub, len(others), 0) + jnp.where(me < n - 1, 1, 0) + jnp.where(me > 0, 1, 0),
+        2 + jnp.where(hub, len(others), 0) + jnp.where(me < n - 1, 1, 0) + jnp.where(me > 0, 1, 0)
+        + jnp.where(relay, 1, 0) + jnp.where(far, 1, 0),
     )
 
     def remote(src, dst, send, recv, peer):
@@ -109,14 +123,23 @@
         here = (others[d], k, pl.ds(p * tok, tok), pl.ds(skip, rows - skip))
         return remote(xs.at[here], lx.at[here], xz_s.at[p, d, k], xz_r.at[p, d, k], z_peer)
 
+    def l_copy(j):
+        return remote(ls.at[j], lr.at[j], l_s.at[j], l_r.at[j], y_peer)
+
     def z_copy(j):
         return remote(zs.at[j], zr.at[j], z_s.at[j], z_r.at[j], z_peer)
 
     def y_copy(j):
         return remote(ys.at[j], yr.at[j], y_s.at[j], y_r.at[j], y_peer)
 
+    def e_copy(j):
+        return remote(es.at[j], er.at[j], e_s.at[j], e_r.at[j], y_peer)
+
     def p_copy(j):
         return remote(kv.at[j], prior.at[j], p_s.at[j], p_r.at[j], right)
+
+    def r_copy(j):
+        return remote(kx.at[j], prior.at[j], r_s.at[j], p_r.at[j], lax.rem(me + 2, n))
 
     for j in range(pieces):
         w_loads[j].wait()
@@ -212,7 +235,6 @@
         loop(0, pieces // 2, take_hub)
         loop(0, LEAD, pass_leaf)
         loop(pieces // 2, pieces, take_hub)
-        pass_leaf(LEAD)
         for s in range(slots):
             for g in others + [grp]:
                 for k in range(2):
@@ -251,113 +273,202 @@
             acc[j] = dot(xs[grp, 0], wbuf[j, grp, 0]) + dot(xs[grp, 1], wbuf[j, grp, 1])
 
         loop(0, pieces, first)
-        if keep:
-            def second(j):
-                value = acc[j]
+        def second(j):
+            value = acc[j]
+            if keep:
                 for d in span:
                     w_keep(j, d).wait_recv()
                     value = value + dot(
                         xs[others[d], 0, :, 0:keep], wbuf[j, others[d], 0, 0:keep]
                     )
                 acc[j] = value
-
-            loop(0, pieces, second)
-
-    def meet(j):
-        @pl.when(hub)
-        def _():
-            for d in span:
-                w_hub(j, 1, d, others[d]).wait_recv()
-            value = jnp.zeros((2 * total, HEAD), jnp.float32)
-            for g in others:
-                value = value + dot(lx[g, 0, :, keep:], wbuf[j, g, 0, keep:])
-                value = value + dot(lx[g, 1], wbuf[j, g, 1])
-            zs[j] = value.astype(jnp.bfloat16)
-            z_copy(j).start()
-            value = acc[j] + dot(xs[grp, 1], wbuf[j, grp, 1])
-            for g in others:
-                value = value + dot(xs[g, 1], wbuf[j, g, 1])
-            acc[j] = value
             ys[j] = value[total:].astype(jnp.bfloat16)
             y_copy(j).start()
 
-            @pl.when(j + LEAD + 1 < pieces)
-            def _():
-                pass_leaf(j + LEAD + 1)
-
-        @pl.when(leaf)
-        def _():
-            z_copy(j).wait_recv()
-            value = acc[j] + zr[j].astype(jnp.float32)
-            acc[j] = value
-            ys[j] = value[total:].astype(jnp.bfloat16)
-            y_copy(j).start()
-
-    def finish(j):
+        loop(0, pieces, second)
+
+    def send_prior(j):
+        @pl.when(me < n - 1)
+        def _():
+            p_copy(j).start()
+
+    def cross_over(j):
+        @pl.when(cross & (j % 2 == 1))
+        def _():
+            p_copy(j).start()
+
+        @pl.when(relay & (j % 2 == 0))
+        def _():
+            r_copy(j).start()
+
+    def meet_hub(j):
+        for d in span:
+            w_hub(j, 1, d, others[d]).wait_recv()
+        part = jnp.zeros((2 * total, HEAD), jnp.float32)
+        for g in others:
+            part = part + dot(lx[g, 0, :, keep:], wbuf[j, g, 0, keep:])
+            part = part + dot(lx[g, 1], wbuf[j, g, 1])
+        ls[j] = part[total:].astype(jnp.bfloat16)
+        l_copy(j).start()
+        value = acc[j] + dot(xs[grp, 1], wbuf[j, grp, 1])
+        for g in others:
+            value = value + dot(xs[g, 1], wbuf[j, g, 1])
+        ys[j] = value[total:].astype(jnp.bfloat16)
+        y_copy(j).start()
+        acc[j, 0:total] = value[:total]
+        acc[j, total:] = part[:total]
+
+        @pl.when(cross & (j % 2 == 0))
+        def _():
+            es[j] = value[:total].astype(jnp.bfloat16)
+            e_copy(j).start()
+
+        @pl.when(relay & (j % 2 == 0))
+        def _():
+            side[j] = value[total:]
+
+    def settle_hub(j):
+        l_copy(j).wait_recv()
+        zs[j] = (acc[j, total:] + lr[j].astype(jnp.float32)).astype(jnp.bfloat16)
+        z_copy(j).start()
         y_copy(j).wait_recv()
         kv[j] = (acc[j, 0:total] + yr[j].astype(jnp.float32)).astype(jnp.bfloat16)
 
-        @pl.when(me < n - 1)
-        def _():
-            p_copy(j).start()
-
-    key_pos = lax.broadcasted_iota(jnp.int32, (tok, 2 * tok), 1) + (me - 1) * tok
-    query_pos = lax.broadcasted_iota(jnp.int32, (tok, 2 * tok), 0) + me * tok
+        @pl.when(jnp.logical_not(cross))
+        def _():
+            send_prior(j)
+
+        @pl.when(relay & (j % 2 == 0))
+        def _():
+            e_copy(j).wait_recv()
+            kx[j] = (side[j] + er[j].astype(jnp.float32)).astype(jnp.bfloat16)
+
+        held = pieces - LEAD - 2
+
+        @pl.when((j < EARLY) | (j > held))
+        def _():
+            cross_over(j)
+
+        @pl.when(j == held)
+        def _():
+            loop(EARLY, held + 1, cross_over)
+
+    def meet_leaf(j):
+        y_copy(j).wait_recv()
+        z_copy(j).wait_recv()
+        kv[j] = (
+            acc[j, 0:total] + yr[j].astype(jnp.float32) + zr[j].astype(jnp.float32)
+        ).astype(jnp.bfloat16)
+        send_prior(j)
+
+    lane = lax.broadcasted_iota(jnp.int32, (tok, tok), 1)
+    own = lane <= lax.broadcasted_iota(jnp.int32, (tok, tok), 0)
+    key_pos = lane + jnp.where(own, me, me - 1) * tok
     wide = q_per_kv * HEAD
 
     def out_copy(h):
         cols = pl.ds(pl.multiple_of(h * wide, HEAD), wide)
         return pltpu.make_async_copy(o_v.at[:, :, cols], o_hbm.at[0, :, :, cols], lo_sem.at[h])
 
-    def attend(h):
+    def wait_prior(j):
         @pl.when(me > 0)
         def _():
-            p_copy(2 * h).wait_recv()
-            p_copy(2 * h + 1).wait_recv()
-
+            p_copy(j).wait_recv()
+
+    def weigh(h):
+        wait_prior(2 * h)
         for s in range(slots):
             here = slice(s * tok, (s + 1) * tok)
             keys = jnp.concatenate([prior[2 * h, here], kv[2 * h, here]], axis=0)
-            values = jnp.concatenate([prior[2 * h + 1, here], kv[2 * h + 1, here]], axis=0)
-            allowed = (key_pos >= start_s[s][:, 0:1]) & (key_pos <= query_pos)
+            allowed = key_pos >= start_s[s]
             for q in range(q_per_kv):
                 cols = pl.ds(pl.multiple_of((h * q_per_kv + q) * HEAD, HEAD), HEAD)
-                scores = lax.dot_general(
+                both = lax.dot_general(
                     q_v[s, :, cols], keys, (((1,), (1,)), ((), ())),
                     preferred_element_type=jnp.float32,
-                ) * HEAD ** (-0.5)
+                )
+                scores = jnp.where(own, both[:, tok:], both[:, :tok]) * HEAD ** (-0.5)
                 scores = jnp.where(allowed, scores, -1e30)
                 maxima = jnp.max(scores, axis=-1, keepdims=True)
-                exponent = jnp.where(allowed, jnp.exp(scores - maxima), 0.0)
+                exponent = jnp.exp(scores - maxima)
                 sums = jnp.sum(exponent, axis=-1, keepdims=True)
-                soft = (exponent / sums).astype(jnp.bfloat16)
-                o_v[s, :, cols] = dot(soft, values).astype(jnp.bfloat16)
+                soft = exponent * (1.0 / sums)
+                weights[s, q, :, 0:tok] = jnp.where(own, 0.0, soft).astype(jnp.bfloat16)
+                weights[s, q, :, tok:] = jnp.where(own, soft, 0.0).astype(jnp.bfloat16)
+
+    def mix(h):
+        wait_prior(2 * h + 1)
+        for s in range(slots):
+            here = slice(s * tok, (s + 1) * tok)
+            values = jnp.concatenate([prior[2 * h + 1, here], kv[2 * h + 1, here]], axis=0)
+            for q in range(q_per_kv):
+                cols = pl.ds(pl.multiple_of((h * q_per_kv + q) * HEAD, HEAD), HEAD)
+                o_v[s, :, cols] = dot(weights[s, q], values).astype(jnp.bfloat16)
         out_copy(h).start()
 
-    def round_of(h):
-        meet(2 * h)
-        finish(2 * h)
-        meet(2 * h + 1)
-
-        @pl.when(h > 0)
-        def _():
-            attend(h - 1)
-
-        finish(2 * h + 1)
-
-    loop(0, heads, round_of)
-    attend(heads - 1)
+    @pl.when(hub)
+    def _():
+        first_late = jnp.where(far, EARLY // 2, heads - LAG)
+
+        def step(j):
+            meet_hub(j)
+
+            @pl.when(j + LEAD < pieces)
+            def _():
+                pass_leaf(j + LEAD)
+
+            @pl.when(j > 0)
+            def _():
+                settle_hub(j - 1)
+
+            @pl.when((j % 2 == 1) & (j > 2 * LAG) & (j // 2 - LAG < first_late))
+            def _():
+                weigh(j // 2 - LAG)
+                mix(j // 2 - LAG)
+
+        loop(0, pieces, step)
+        settle_hub(pieces - 1)
+
+        def rest(h):
+            weigh(h)
+            mix(h)
+
+        loop(first_late, heads, rest)
+
+    @pl.when(leaf)
+    def _():
+        def step(h):
+            meet_leaf(2 * h)
+
+            @pl.when(h > 0)
+            def _():
+                mix(h - 1)
+
+            weigh(h)
+            meet_leaf(2 * h + 1)
+
+        loop(0, heads, step)
+        mix(heads - 1)
 
     def drain(j):
         y_copy(j).wait_send()
 
-        @pl.when(me < n - 1)
+        @pl.when((me < n - 1) & jnp.logical_not(cross & (j % 2 == 0)))
         def _():
             p_copy(j).wait_send()
 
+        @pl.when(cross & (j % 2 == 0))
+        def _():
+            e_copy(j).wait_send()
+
+        @pl.when(relay & (j % 2 == 0))
+        def _():
+            r_copy(j).wait_send()
+
         @pl.when(hub)
         def _():
             w_pair(j, 0).wait_send()
+            l_copy(j).wait_send()
             z_copy(j).wait_send()
             for d in span:
                 w_hub(j, 0, d, grp).wait_send()
@@ -414,12 +525,19 @@
             pltpu.VMEM((groups, 2, total, rows), bf),
             pltpu.VMEM((groups, 2, 2 * total, rows), bf),
             pltpu.VMEM((pieces, 2 * total, HEAD), f32),
-            pltpu.VMEM((pieces, 2 * total, HEAD), bf),
-            pltpu.VMEM((pieces, 2 * total, HEAD), bf),
-            pltpu.VMEM((pieces, total, HEAD), bf),
-            pltpu.VMEM((pieces, total, HEAD), bf),
-            pltpu.VMEM((pieces, total, HEAD), bf),
-            pltpu.VMEM((pieces, total, HEAD), bf),
+            pltpu.VMEM((pieces, total, HEAD), bf),
+            pltpu.VMEM((pieces, total, HEAD), bf),
+            pltpu.VMEM((pieces, total, HEAD), bf),
+            pltpu.VMEM((pieces, total, HEAD), bf),
+            pltpu.VMEM((pieces, total, HEAD), bf),
+            pltpu.VMEM((pieces, total, HEAD), bf),
+            pltpu.VMEM((pieces, total, HEAD), bf),
+            pltpu.VMEM((pieces, total, HEAD), bf),
+            pltpu.VMEM((pieces, total, HEAD), bf),
+            pltpu.VMEM((pieces, total, HEAD), bf),
+            pltpu.VMEM((pieces, total, HEAD), bf),
+            pltpu.VMEM((pieces, total, HEAD), f32),
+            pltpu.VMEM((slots, queries.shape[-1] // key_width, tok, 2 * tok), bf),
             pltpu.VMEM((slots, tok, HEAD), jnp.int32),
             dma((pieces,)), dma((slots,)), dma, dma((heads,)),
             dma((pieces,)), dma((pieces,)),
@@ -430,6 +548,8 @@
             dma((pieces,)), dma((pieces,)),
             dma((pieces,)), dma((pieces,)),
             dma((pieces,)), dma((pieces,)),
+            dma((pieces,)), dma((pieces,)),
+            dma((pieces,)), dma((pieces,)), dma((pieces,)),
         ],
         compiler_params=pltpu.CompilerParams(
             collective_id=0, has_side_effects=True, vmem_limit_bytes=60 * 1024 * 1024

time: 125 us -> 117 us (0.936); the launches traced: 123 us -> 117 us
  Pallas kernels: 120 us -> 114 us
    pallas_call x1, Pallas kernels: 120 us -> 114 us  [body(): pl.pallas_call(functools.partial(kernel, n, keep), out_shape=jax.ShapeDty...]
where the time goes in v2:
time: 117 us
  Pallas kernels  114 us (97%)
  local copies, waits for them, and re-layouts  3.13 us (3%)
    pallas_call x1, Pallas kernels, body(): pl.pallas_call(functools.partial(kernel, n, keep), out_shape=jax.ShapeDty...  114 us
    unnamed x1, local copies, waits for them, and re-layouts  3.13 us

profile of v2, /device:TPU:8, one launch (start us, length us, event | category | flops | bytes accessed | tf_op | source)
XLA Modules:
  0.0 116.6 jit_solution(12182477596265832884)
XLA Ops:
  0.0 113.5 %shard_map.64 = bf16[1,2,128,4096]{3,2,1,0:T(8,128)(2,1)} custom-call(bf16[1,2,128,8192]{3,2,1,0:T(8,128)(2,1)} %x_hbm.1, bf16[1,2,128,4096]{3,2,1,0:T(8,128)(2,1)} %q_hbm.1, bf16[1,8192]{1,0:T(2,128)(2,1)} %gain_ref.1, bf16[1,1024,512]{2,1,0:T(8,128)(2,1)} %kw_hbm.1, bf16[1,1024,512]{2,1,0:T(8,128)(2,1)} %vw_hbm.1, s32[2,16]{1,0:T(2,128)} %len_ref.1), custom_call_target="tpu_custom_call" | custom-call | tf_op jit(solution)/shard_map/pallas_call | solution.py:514
  113.5 3.1 %copy.8 = bf16[1,2,128,4096]{3,2,1,0:T(8,128)(2,1)} copy(bf16[1,2,128,4096]{3,2,1,0:T(8,128)(2,1)} %shard_map.64) | data formatting | bytes 4194304

commit v3 on v2

--- a/solution.py
+++ b/solution.py
@@ -17,10 +17,10 @@
 def kernel(
     n, keep,
     x_hbm, q_hbm, gain_ref, kw_hbm, vw_hbm, len_ref, o_hbm,
-    x_v, q_v, o_v, wbuf, xs, sx, lx, acc, ls, lr, zs, zr, ys, yr, es, er, kv, kx, prior, side, weights, start_s,
+    x_v, q_v, o_v, wbuf, xs, sx, lx, acc, ls, lr, zs, zr, ys, yr, es, er, fs, fr, kv, kx, kq, prior, side, behind, part_s, weights, start_s,
     lw_sem, lx_sem, lq_sem, lo_sem,
     wz_s, wz_r, wh_s, wh_r, wk_s, wk_r, xy_s, xy_r, xz_s, xz_r,
-    l_s, l_r, z_s, z_r, y_s, y_r, e_s, e_r, p_s, p_r, r_s,
+    l_s, l_r, z_s, z_r, y_s, y_r, e_s, e_r, f_s, f_r, p_s, p_r, q_s, q_r, r_s,
 ):
     slots, tok, depth = x_v.shape
     pieces, groups, _, rows, _ = wbuf.shape
@@ -43,6 +43,10 @@
     cross = (me % 4 == 3) & (grp % 2 == 0) & (me < n - 1)
     relay = (me % 4 == 2) & (grp % 2 == 0) & (me < n - 2)
     far = (me % 4 == 0) & (grp % 2 == 1)
+    base = (me % 4 == 0) & (grp % 2 == 0)
+    rear = (me % 4 == 1) & (grp % 2 == 0)
+    front = (me % 4 == 2) & (grp % 2 == 0)
+    mate = (me % 4 == 3) & (grp % 2 == 0)
 
     def hub_of(g):
         return 4 * g + 2 * (1 - g % 2) + bit
@@ -134,6 +138,12 @@
 
     def e_copy(j):
         return remote(es.at[j], er.at[j], e_s.at[j], e_r.at[j], y_peer)
+
+    def f_copy(j):
+        return remote(fs.at[j], fr.at[j], f_s.at[j], f_r.at[j], y_peer)
+
+    def q_copy(j):
+        return remote(kx.at[j], kq.at[j], q_s.at[j], q_r.at[j], z_peer)
 
     def p_copy(j):
         return remote(kv.at[j], prior.at[j], p_s.at[j], p_r.at[j], right)
@@ -285,10 +295,15 @@
             ys[j] = value[total:].astype(jnp.bfloat16)
             y_copy(j).start()
 
+            @pl.when(rear)
+            def _():
+                es[j] = value[:total].astype(jnp.bfloat16)
+                e_copy(j).start()
+
         loop(0, pieces, second)
 
     def send_prior(j):
-        @pl.when(me < n - 1)
+        @pl.when((me < n - 1) & jnp.logical_not(cross) & jnp.logical_not(rear))
         def _():
             p_copy(j).start()
 
@@ -301,16 +316,22 @@
         def _():
             r_copy(j).start()
 
+    held = pieces - LEAD - 2
+
     def meet_hub(j):
-        for d in span:
-            w_hub(j, 1, d, others[d]).wait_recv()
         part = jnp.zeros((2 * total, HEAD), jnp.float32)
         for g in others:
             part = part + dot(lx[g, 0, :, keep:], wbuf[j, g, 0, keep:])
+        part_s[...] = part
+        acc[j] = acc[j] + dot(xs[grp, 1], wbuf[j, grp, 1])
+        for d in span:
+            w_hub(j, 1, d, others[d]).wait_recv()
+        part = part_s[...]
+        for g in others:
             part = part + dot(lx[g, 1], wbuf[j, g, 1])
         ls[j] = part[total:].astype(jnp.bfloat16)
         l_copy(j).start()
-        value = acc[j] + dot(xs[grp, 1], wbuf[j, grp, 1])
+        value = acc[j]
         for g in others:
             value = value + dot(xs[g, 1], wbuf[j, g, 1])
         ys[j] = value[total:].astype(jnp.bfloat16)
@@ -318,10 +339,19 @@
         acc[j, 0:total] = value[:total]
         acc[j, total:] = part[:total]
 
+        @pl.when(mate)
+        def _():
+            fs[j] = part[:total].astype(jnp.bfloat16)
+            f_copy(j).start()
+
         @pl.when(cross & (j % 2 == 0))
         def _():
             es[j] = value[:total].astype(jnp.bfloat16)
             e_copy(j).start()
+
+        @pl.when(front)
+        def _():
+            behind[j] = part[total:]
 
         @pl.when(relay & (j % 2 == 0))
         def _():
@@ -333,18 +363,13 @@
         z_copy(j).start()
         y_copy(j).wait_recv()
         kv[j] = (acc[j, 0:total] + yr[j].astype(jnp.float32)).astype(jnp.bfloat16)
-
-        @pl.when(jnp.logical_not(cross))
-        def _():
-            send_prior(j)
+        send_prior(j)
 
         @pl.when(relay & (j % 2 == 0))
         def _():
             e_copy(j).wait_recv()
             kx[j] = (side[j] + er[j].astype(jnp.float32)).astype(jnp.bfloat16)
 
-        held = pieces - LEAD - 2
-
         @pl.when((j < EARLY) | (j > held))
         def _():
             cross_over(j)
@@ -353,12 +378,20 @@
         def _():
             loop(EARLY, held + 1, cross_over)
 
+    def gather_leaf(j):
+        y_copy(j).wait_recv()
+        value = acc[j, 0:total] + yr[j].astype(jnp.float32)
+        acc[j, 0:total] = value
+
+        @pl.when(base)
+        def _():
+            e_copy(j).wait_recv()
+            kx[j] = (acc[j, total:] + er[j].astype(jnp.float32)).astype(jnp.bfloat16)
+            q_copy(j).start()
+
     def meet_leaf(j):
-        y_copy(j).wait_recv()
         z_copy(j).wait_recv()
-        kv[j] = (
-            acc[j, 0:total] + yr[j].astype(jnp.float32) + zr[j].astype(jnp.float32)
-        ).astype(jnp.bfloat16)
+        kv[j] = (acc[j, 0:total] + zr[j].astype(jnp.float32)).astype(jnp.bfloat16)
         send_prior(j)
 
     lane = lax.broadcasted_iota(jnp.int32, (tok, tok), 1)
@@ -371,9 +404,17 @@
         return pltpu.make_async_copy(o_v.at[:, :, cols], o_hbm.at[0, :, :, cols], lo_sem.at[h])
 
     def wait_prior(j):
-        @pl.when(me > 0)
+        @pl.when((me > 0) & jnp.logical_not(front))
         def _():
             p_copy(j).wait_recv()
+
+        @pl.when(front)
+        def _():
+            q_copy(j).wait_recv()
+            f_copy(j).wait_recv()
+            prior[j] = (
+                behind[j] + kq[j].astype(jnp.float32) + fr[j].astype(jnp.float32)
+            ).astype(jnp.bfloat16)
 
     def weigh(h):
         wait_prior(2 * h)
@@ -447,17 +488,26 @@
             weigh(h)
             meet_leaf(2 * h + 1)
 
+        loop(0, pieces, gather_leaf)
         loop(0, heads, step)
         mix(heads - 1)
 
     def drain(j):
         y_copy(j).wait_send()
 
-        @pl.when((me < n - 1) & jnp.logical_not(cross & (j % 2 == 0)))
+        @pl.when((me < n - 1) & jnp.logical_not(cross & (j % 2 == 0)) & jnp.logical_not(rear))
         def _():
             p_copy(j).wait_send()
 
-        @pl.when(cross & (j % 2 == 0))
+        @pl.when(base)
+        def _():
+            q_copy(j).wait_send()
+
+        @pl.when(mate)
+        def _():
+            f_copy(j).wait_send()
+
+        @pl.when((cross & (j % 2 == 0)) | rear)
         def _():
             e_copy(j).wait_send()
 
@@ -536,7 +586,12 @@
             pltpu.VMEM((pieces, total, HEAD), bf),
             pltpu.VMEM((pieces, total, HEAD), bf),
             pltpu.VMEM((pieces, total, HEAD), bf),
+            pltpu.VMEM((pieces, total, HEAD), bf),
+            pltpu.VMEM((pieces, total, HEAD), bf),
+            pltpu.VMEM((pieces, total, HEAD), bf),
             pltpu.VMEM((pieces, total, HEAD), f32),
+            pltpu.VMEM((pieces, total, HEAD), f32),
+            pltpu.VMEM((2 * total, HEAD), f32),
             pltpu.VMEM((slots, queries.shape[-1] // key_width, tok, 2 * tok), bf),
             pltpu.VMEM((slots, tok, HEAD), jnp.int32),
             dma((pieces,)), dma((slots,)), dma, dma((heads,)),
@@ -549,6 +604,7 @@
             dma((pieces,)), dma((pieces,)),
             dma((pieces,)), dma((pieces,)),
             dma((pieces,)), dma((pieces,)),
+            dma((pieces,)), dma((pieces,)), dma((pieces,)), dma((pieces,)),
             dma((pieces,)), dma((pieces,)), dma((pieces,)),
         ],
         compiler_params=pltpu.CompilerParams(

time: 117 us -> 113 us (0.966)
  the two profiles are of different devices: /device:TPU:8 before, /device:TPU:28 now
where the time goes in v3:
time: 113 us
  Pallas kernels  110 us (97%)
  local copies, waits for them, and re-layouts  3.13 us (3%)
    pallas_call x1, Pallas kernels, body(): pl.pallas_call(functools.partial(kernel, n, keep), out_shape=jax.ShapeDty...  110 us
    unnamed x1, local copies, waits for them, and re-layouts  3.13 us

profile of v3, /device:TPU:28, one launch (start us, length us, event | category | flops | bytes accessed | tf_op | source)
XLA Modules:
  0.0 113.1 jit_solution(9984269146198907131)
XLA Ops:
  0.0 110.0 %shard_map.64 = bf16[1,2,128,4096]{3,2,1,0:T(8,128)(2,1)} custom-call(bf16[1,2,128,8192]{3,2,1,0:T(8,128)(2,1)} %x_hbm.1, bf16[1,2,128,4096]{3,2,1,0:T(8,128)(2,1)} %q_hbm.1, bf16[1,8192]{1,0:T(2,128)(2,1)} %gain_ref.1, bf16[1,1024,512]{2,1,0:T(8,128)(2,1)} %kw_hbm.1, bf16[1,1024,512]{2,1,0:T(8,128)(2,1)} %vw_hbm.1, s32[2,16]{1,0:T(2,128)} %len_ref.1), custom_call_target="tpu_custom_call" | custom-call | tf_op jit(solution)/shard_map/pallas_call | solution.py:564
  110.0 3.1 %copy.8 = bf16[1,2,128,4096]{3,2,1,0:T(8,128)(2,1)} copy(bf16[1,2,128,4096]{3,2,1,0:T(8,128)(2,1)} %shard_map.64) | data formatting | bytes 4194304

commit v4 on v3

--- a/solution.py
+++ b/solution.py
@@ -11,16 +11,16 @@
 AXIS = "fsdp"
 LEAD = 2
 LAG = 2
-EARLY = 2
+EARLY = 0
 
 
 def kernel(
     n, keep,
     x_hbm, q_hbm, gain_ref, kw_hbm, vw_hbm, len_ref, o_hbm,
-    x_v, q_v, o_v, wbuf, xs, sx, lx, acc, ls, lr, zs, zr, ys, yr, es, er, fs, fr, kv, kx, kq, prior, side, behind, part_s, weights, start_s,
+    x_v, q_v, o_v, wbuf, xs, sx, lx, acc, ls, lr, zs, zr, ys, yr, es, er, fs, fr, kv, kx, kq, prior, side, behind, part_s, us, ua, ub, weights, start_s,
     lw_sem, lx_sem, lq_sem, lo_sem,
     wz_s, wz_r, wh_s, wh_r, wk_s, wk_r, xy_s, xy_r, xz_s, xz_r,
-    l_s, l_r, z_s, z_r, y_s, y_r, e_s, e_r, f_s, f_r, p_s, p_r, q_s, q_r, r_s,
+    l_s, l_r, z_s, z_r, y_s, y_r, e_s, e_r, f_s, f_r, p_s, p_r, q_s, q_r, r_s, u_s, u_r,
 ):
     slots, tok, depth = x_v.shape
     pieces, groups, _, rows, _ = wbuf.shape
@@ -36,6 +36,8 @@
     kind = jnp.where(leaf, 1, 0)
     y_peer = me + 1 - 2 * bit
     z_peer = me + 2 - 4 * cls
+    diagonal = z_peer + 1 - 2 * bit
+    final = pieces - 1
     right = lax.rem(me + 1, n)
     left = lax.rem(me + n - 1, n)
     others = [lax.rem(grp + d, groups) for d in range(1, groups)]
@@ -69,6 +71,7 @@
 
     greet(y_peer)
     greet(z_peer)
+    greet(diagonal)
 
     @pl.when(hub)
     def _():
@@ -94,7 +97,7 @@
     prior[...] = jnp.zeros_like(prior)
     pl.semaphore_wait(
         barrier,
-        2 + jnp.where(hub, len(others), 0) + jnp.where(me < n - 1, 1, 0) + jnp.where(me > 0, 1, 0)
+        3 + jnp.where(hub, len(others), 0) + jnp.where(me < n - 1, 1, 0) + jnp.where(me > 0, 1, 0)
         + jnp.where(relay, 1, 0) + jnp.where(far, 1, 0),
     )
 
@@ -144,6 +147,15 @@
 
     def q_copy(j):
         return remote(kx.at[j], kq.at[j], q_s.at[j], q_r.at[j], z_peer)
+
+    def near(size):
+        rows_of = pl.ds(0, size)
+        return remote(us.at[rows_of], ua.at[rows_of], u_s.at[0], u_r.at[0], z_peer)
+
+    def slant(first, size):
+        return remote(
+            us.at[pl.ds(first, size)], ub.at[pl.ds(0, size)], u_s.at[1], u_r.at[1], diagonal
+        )
 
     def p_copy(j):
         return remote(kv.at[j], prior.at[j], p_s.at[j], p_r.at[j], right)
@@ -295,7 +307,7 @@
             ys[j] = value[total:].astype(jnp.bfloat16)
             y_copy(j).start()
 
-            @pl.when(rear)
+            @pl.when(rear | ((bit == 0) & (j == final)))
             def _():
                 es[j] = value[:total].astype(jnp.bfloat16)
                 e_copy(j).start()
@@ -303,7 +315,7 @@
         loop(0, pieces, second)
 
     def send_prior(j):
-        @pl.when((me < n - 1) & jnp.logical_not(cross) & jnp.logical_not(rear))
+        @pl.when((me < n - 1) & jnp.logical_not(cross) & jnp.logical_not(rear | (leaf & (bit == 0) & (j == final))))
         def _():
             p_copy(j).start()
 
@@ -318,7 +330,7 @@
 
     held = pieces - LEAD - 2
 
-    def meet_hub(j):
+    def meet_hub(j, last):
         part = jnp.zeros((2 * total, HEAD), jnp.float32)
         for g in others:
             part = part + dot(lx[g, 0, :, keep:], wbuf[j, g, 0, keep:])
@@ -329,8 +341,21 @@
         part = part_s[...]
         for g in others:
             part = part + dot(lx[g, 1], wbuf[j, g, 1])
-        ls[j] = part[total:].astype(jnp.bfloat16)
-        l_copy(j).start()
+        if last:
+            us[...] = part.astype(jnp.bfloat16)
+
+            @pl.when(bit == 0)
+            def _():
+                slant(0, 2 * total).start()
+                near(total).start()
+
+            @pl.when(bit == 1)
+            def _():
+                near(2 * total).start()
+                slant(total, total).start()
+        else:
+            ls[j] = part[total:].astype(jnp.bfloat16)
+            l_copy(j).start()
         value = acc[j]
         for g in others:
             value = value + dot(xs[g, 1], wbuf[j, g, 1])
@@ -357,10 +382,11 @@
         def _():
             side[j] = value[total:]
 
-    def settle_hub(j):
-        l_copy(j).wait_recv()
-        zs[j] = (acc[j, total:] + lr[j].astype(jnp.float32)).astype(jnp.bfloat16)
-        z_copy(j).start()
+    def settle_hub(j, last=False):
+        if not last:
+            l_copy(j).wait_recv()
+            zs[j] = (acc[j, total:] + lr[j].astype(jnp.float32)).astype(jnp.bfloat16)
+            z_copy(j).start()
         y_copy(j).wait_recv()
         kv[j] = (acc[j, 0:total] + yr[j].astype(jnp.float32)).astype(jnp.bfloat16)
         send_prior(j)
@@ -383,6 +409,11 @@
         value = acc[j, 0:total] + yr[j].astype(jnp.float32)
         acc[j, 0:total] = value
 
+        @pl.when((bit == 1) & (j == final))
+        def _():
+            e_copy(j).wait_recv()
+            acc[j, total:] = acc[j, total:] + er[j].astype(jnp.float32)
+
         @pl.when(base)
         def _():
             e_copy(j).wait_recv()
@@ -394,6 +425,26 @@
         kv[j] = (acc[j, 0:total] + zr[j].astype(jnp.float32)).astype(jnp.bfloat16)
         send_prior(j)
 
+    def last_leaf():
+        def sums(mine, other):
+            value = acc[final, mine:mine + total] + ua[mine:mine + total].astype(jnp.float32)
+            return (value + ub[other:other + total].astype(jnp.float32)).astype(jnp.bfloat16)
+
+        @pl.when(bit == 0)
+        def _():
+            near(total).wait_recv()
+            slant(total, total).wait_recv()
+            kv[final] = sums(0, 0)
+
+        @pl.when(bit == 1)
+        def _():
+            near(2 * total).wait_recv()
+            slant(0, 2 * total).wait_recv()
+            kv[final] = sums(0, total)
+            prior[final] = sums(total, 0)
+
+        send_prior(final)
+
     lane = lax.broadcasted_iota(jnp.int32, (tok, tok), 1)
     own = lane <= lax.broadcasted_iota(jnp.int32, (tok, tok), 0)
     key_pos = lane + jnp.where(own, me, me - 1) * tok
@@ -404,7 +455,7 @@
         return pltpu.make_async_copy(o_v.at[:, :, cols], o_hbm.at[0, :, :, cols], lo_sem.at[h])
 
     def wait_prior(j):
-        @pl.when((me > 0) & jnp.logical_not(front))
+        @pl.when((me > 0) & jnp.logical_not(front | (leaf & (bit == 1) & (j == final))))
         def _():
             p_copy(j).wait_recv()
 
@@ -452,7 +503,7 @@
         first_late = jnp.where(far, EARLY // 2, heads - LAG)
 
         def step(j):
-            meet_hub(j)
+            meet_hub(j, False)
 
             @pl.when(j + LEAD < pieces)
             def _():
@@ -467,8 +518,16 @@
                 weigh(j // 2 - LAG)
                 mix(j // 2 - LAG)
 
-        loop(0, pieces, step)
-        settle_hub(pieces - 1)
+        loop(0, final, step)
+
+        @pl.when(first_late == heads - LAG)
+        def _():
+            weigh(heads - 1 - LAG)
+            mix(heads - 1 - LAG)
+
+        settle_hub(final - 1)
+        meet_hub(final, True)
+        settle_hub(final, True)
 
         def rest(h):
             weigh(h)
@@ -486,16 +545,22 @@
                 mix(h - 1)
 
             weigh(h)
-            meet_leaf(2 * h + 1)
+
+            @pl.when(2 * h + 1 < final)
+            def _():
+                meet_leaf(2 * h + 1)
 
         loop(0, pieces, gather_leaf)
         loop(0, heads, step)
+        last_leaf()
         mix(heads - 1)
 
     def drain(j):
         y_copy(j).wait_send()
 
-        @pl.when((me < n - 1) & jnp.logical_not(cross & (j % 2 == 0)) & jnp.logical_not(rear))
+        @pl.when((me < n - 1) & jnp.logical_not(
+            (cross & (j % 2 == 0)) | rear | (leaf & (bit == 0) & (j == final))
+        ))
         def _():
             p_copy(j).wait_send()
 
@@ -507,7 +572,7 @@
         def _():
             f_copy(j).wait_send()
 
-        @pl.when((cross & (j % 2 == 0)) | rear)
+        @pl.when((cross & (j % 2 == 0)) | rear | (leaf & (bit == 0) & (j == final)))
         def _():
             e_copy(j).wait_send()
 
@@ -518,8 +583,12 @@
         @pl.when(hub)
         def _():
             w_pair(j, 0).wait_send()
-            l_copy(j).wait_send()
-            z_copy(j).wait_send()
+
+            @pl.when(j < final)
+            def _():
+                l_copy(j).wait_send()
+                z_copy(j).wait_send()
+
             for d in span:
                 w_hub(j, 0, d, grp).wait_send()
                 w_hub(j, 1, d, grp).wait_send()
@@ -531,6 +600,17 @@
             w_pair(j, 1).wait_send()
 
     loop(0, pieces, drain)
+
+    @pl.when(hub & (bit == 0))
+    def _():
+        slant(0, 2 * total).wait_send()
+        near(total).wait_send()
+
+    @pl.when(hub & (bit == 1))
+    def _():
+        near(2 * total).wait_send()
+        slant(total, total).wait_send()
+
     for s in range(slots):
         for g in range(groups):
             for k in range(2):
@@ -592,6 +672,9 @@
             pltpu.VMEM((pieces, total, HEAD), f32),
             pltpu.VMEM((pieces, total, HEAD), f32),
             pltpu.VMEM((2 * total, HEAD), f32),
+            pltpu.VMEM((2 * total, HEAD), bf),
+            pltpu.VMEM((2 * total, HEAD), bf),
+            pltpu.VMEM((2 * total, HEAD), bf),
             pltpu.VMEM((slots, queries.shape[-1] // key_width, tok, 2 * tok), bf),
             pltpu.VMEM((slots, tok, HEAD), jnp.int32),
             dma((pieces,)), dma((slots,)), dma, dma((heads,)),
@@ -606,6 +689,7 @@
             dma((pieces,)), dma((pieces,)),
             dma((pieces,)), dma((pieces,)), dma((pieces,)), dma((pieces,)),
             dma((pieces,)), dma((pieces,)), dma((pieces,)),
+            dma((2,)), dma((2,)),
         ],
         compiler_params=pltpu.CompilerParams(
             collective_id=0, has_side_effects=True, vmem_limit_bytes=60 * 1024 * 1024

time: 113 us -> 112 us (level)
  the two profiles are of different devices: /device:TPU:28 before, /device:TPU:8 now
where the time goes in v4:
time: 112 us; the launch traced here: 110 us
  Pallas kernels  107 us (96%)
  local copies, waits for them, and re-layouts  3.13 us (3%)
    pallas_call x1, Pallas kernels, body(): pl.pallas_call(functools.partial(kernel, n, keep), out_shape=jax.ShapeDty...  107 us
    unnamed x1, local copies, waits for them, and re-layouts  3.13 us

profile of v4, /device:TPU:8, one launch (start us, length us, event | category | flops | bytes accessed | tf_op | source)
XLA Modules:
  0.0 109.9 jit_solution(11358828065869801415)
XLA Ops:
  0.0 106.8 %shard_map.64 = bf16[1,2,128,4096]{3,2,1,0:T(8,128)(2,1)} custom-call(bf16[1,2,128,8192]{3,2,1,0:T(8,128)(2,1)} %x_hbm.1, bf16[1,2,128,4096]{3,2,1,0:T(8,128)(2,1)} %q_hbm.1, bf16[1,8192]{1,0:T(2,128)(2,1)} %gain_ref.1, bf16[1,1024,512]{2,1,0:T(8,128)(2,1)} %kw_hbm.1, bf16[1,1024,512]{2,1,0:T(8,128)(2,1)} %vw_hbm.1, s32[2,16]{1,0:T(2,128)} %len_ref.1), custom_call_target="tpu_custom_call" | custom-call | tf_op jit(solution)/shard_map/pallas_call | solution.py:644
  106.8 3.1 %copy.8 = bf16[1,2,128,4096]{3,2,1,0:T(8,128)(2,1)} copy(bf16[1,2,128,4096]{3,2,1,0:T(8,128)(2,1)} %shard_map.64) | data formatting | bytes 4194304

commit v5 on v4

--- a/solution.py
+++ b/solution.py
@@ -527,13 +527,19 @@
 
         settle_hub(final - 1)
         meet_hub(final, True)
+
+        @pl.when(far)
+        def _():
+            weigh(first_late)
+            mix(first_late)
+
         settle_hub(final, True)
 
         def rest(h):
             weigh(h)
             mix(h)
 
-        loop(first_late, heads, rest)
+        loop(first_late + jnp.where(far, 1, 0), heads, rest)
 
     @pl.when(leaf)
     def _():

time: 112 us -> 112 us (level)
  no operation moved by 1% of the time
where the time goes in v5:
time: 112 us; the launch traced here: 110 us
  Pallas kernels  107 us (96%)
  local copies, waits for them, and re-layouts  3.13 us (3%)
    pallas_call x1, Pallas kernels, body(): pl.pallas_call(functools.partial(kernel, n, keep), out_shape=jax.ShapeDty...  107 us
    unnamed x1, local copies, waits for them, and re-layouts  3.13 us

profile of v5, /device:TPU:8, one launch (start us, length us, event | category | flops | bytes accessed | tf_op | source)
XLA Modules:
  0.0 109.9 jit_solution(4228772185840487946)
XLA Ops:
  0.0 106.7 %shard_map.64 = bf16[1,2,128,4096]{3,2,1,0:T(8,128)(2,1)} custom-call(bf16[1,2,128,8192]{3,2,1,0:T(8,128)(2,1)} %x_hbm.1, bf16[1,2,128,4096]{3,2,1,0:T(8,128)(2,1)} %q_hbm.1, bf16[1,8192]{1,0:T(2,128)(2,1)} %gain_ref.1, bf16[1,1024,512]{2,1,0:T(8,128)(2,1)} %kw_hbm.1, bf16[1,1024,512]{2,1,0:T(8,128)(2,1)} %vw_hbm.1, s32[2,16]{1,0:T(2,128)} %len_ref.1), custom_call_target="tpu_custom_call" | custom-call | tf_op jit(solution)/shard_map/pallas_call | solution.py:650
  106.7 3.1 %copy.8 = bf16[1,2,128,4096]{3,2,1,0:T(8,128)(2,1)} copy(bf16[1,2,128,4096]{3,2,1,0:T(8,128)(2,1)} %shard_map.64) | data formatting | bytes 4194304
